TPU v7x, 256 devices: a whole 4x4x8 slice. The times are simulated.
256 devices in a mesh: dp: 16 (over z, core), feat: 16 (over x, y).
Axes of the slice: x: 4, y: 4, z: 8, core: 2. Of those that a mesh axis runs over, the one named last changes fastest.
Arguments:
- points: bfloat16 [4096, 256], P('dp'), may hold values from -6 to 6
- freqs: bfloat16 [256, 8192], P(None, 'feat'), may hold values from -0.375 to 0.375
- phase: float32 [8192], P('feat'), may hold values from -3.140625 to 3.140625
- ridge: float32 [8192], P('feat'), may hold values from 0.05 to 0.5
- targets: bfloat16 [8, 4096], P(None, 'dp'), may hold values from -6 to 6
Outputs:
- gram: float32 [8192, 8192], P('feat', 'dp')
- projected: float32 [8, 8192], P(None, 'feat')
- factors: float32 [8192, 1024], P('feat')
All inputs are finite; a program needn't handle non-finite values.
Results may differ from a plain program's by a relative error of at most 0.003.
Values may be sent and summed in bfloat16 or wider, within the bound.
A program may use at most 128 MiB of HBM per device.

v0:
```python
import math
import jax
import jax.numpy as jnp
from jax import lax
from jax.sharding import PartitionSpec as P

FB = 1024


def features(rows, freq_cols, phase_cols, scale):
    angle = jnp.dot(rows, freq_cols, preferred_element_type=jnp.float32) + phase_cols
    return (scale * jnp.cos(angle)).astype(jnp.bfloat16)


def cross(left, right):
    return lax.dot_general(
        left, right, (((0,), (0,)), ((), ())), preferred_element_type=jnp.float32
    )


def with_ridge(tile, ridge, row_start, col_start):
    rows_here = row_start + lax.broadcasted_iota(jnp.int32, tile.shape, 0)
    cols_here = col_start + lax.broadcasted_iota(jnp.int32, tile.shape, 1)
    return tile + jnp.where(rows_here == cols_here, ridge[:, None], 0.0)


def shards(points, freqs, phase, ridge, targets):
    data_count = lax.axis_size("dp")
    feat_count = lax.axis_size("feat")
    feat_index = lax.axis_index("feat")
    data_index = lax.axis_index("dp")
    local_width = freqs.shape[1]
    total_width = local_width * feat_count
    tile_width = total_width // data_count
    window = max(local_width, FB)
    window_start = feat_index * local_width // window * window
    row_start = feat_index * local_width
    col_start = data_index * tile_width
    scale = math.sqrt(2.0 / (points.shape[0] * data_count))
    points_all, targets_all = (
        lax.all_gather(points, "dp", axis=0, tiled=True),
        lax.all_gather(targets, "dp", axis=1, tiled=True),
    )
    freqs_wide, phase_all, ridge_all = (
        lax.all_gather(freqs.astype(jnp.float32), "feat", axis=1, tiled=True),
        lax.all_gather(phase, "feat", axis=0, tiled=True),
        lax.all_gather(ridge, "feat", axis=0, tiled=True),
    )
    freqs_all = freqs_wide.astype(jnp.bfloat16)
    row_phi = features(points_all, freqs, phase, scale)
    col_phi = features(
        points_all,
        lax.dynamic_slice_in_dim(freqs_all, col_start, tile_width, 1),
        lax.dynamic_slice_in_dim(phase_all, col_start, tile_width, 0),
        scale,
    )
    gram_tile = cross(row_phi, col_phi)
    window_phi = features(
        points_all,
        lax.dynamic_slice_in_dim(freqs_all, window_start, window, 1),
        lax.dynamic_slice_in_dim(phase_all, window_start, window, 0),
        scale,
    )
    projected = jnp.dot(targets_all, row_phi, preferred_element_type=jnp.float32)
    slab = cross(window_phi, window_phi)
    window_ridge = lax.dynamic_slice_in_dim(ridge_all, window_start, window, 0)
    slab = with_ridge(slab, window_ridge, window_start, window_start)
    gram_tile = with_ridge(gram_tile, ridge, row_start, col_start)
    block_count = window // FB
    stacked = jnp.stack([slab])
    factors_all = jnp.linalg.cholesky(stacked).reshape(window, FB)
    factor_rows = lax.dynamic_slice_in_dim(factors_all, row_start - window_start, local_width, 0)
    return (gram_tile, projected, factor_rows)


def solution(mesh):
    in_specs = (P("dp", None), P(None, "feat"), P("feat"), P("feat"), P(None, "dp"))
    out_specs = (P("feat", "dp"), P(None, "feat"), P("feat", None))
    return jax.shard_map(shards, mesh=mesh, in_specs=in_specs, out_specs=out_specs, check_vma=False)
```

profile of v0, /device:TPU:2, one launch (start us, length us, event | category | flops | bytes accessed | tf_op | source)
XLA Modules:
  0.0 462.8 jit_solution(10146078261034066194)
XLA Ops:
  7.2 0.7 all-gather.5.cloned.1.call-update
  7.9 0.7 all-gather.7.cloned.1.call-update
  8.7 23.4 %all-gather = f32[16,1,512]{2,1,0:T(1,128)S(1)} all-gather(f32[1,1,512]{2,1,0:T(1,128)} %bitcast.188), channel_id=1, replica_groups=mesh['dp'=16,'feat'=16] {'feat'}, dimensions={0}, use_global_device_ids=true | all-gather | bytes 34816 | tf_op jit(solution)/shard_map/all_gather | solution.py:46
  32.1 0.1 dynamic_slice.21
  32.1 21.7 %all-gather.1 = f32[16,1,512]{2,1,0:T(1,128)S(1)} all-gather(f32[1,1,512]{2,1,0:T(1,128)} %bitcast.189), channel_id=1, replica_groups=mesh['dp'=16,'feat'=16] {'feat'}, dimensions={0}, use_global_device_ids=true | all-gather | bytes 34816 | tf_op jit(solution)/shard_map/all_gather | solution.py:47
  53.9 20.4 %all_gather.18 = bf16[8,4096]{1,0:T(8,128)(2,1)S(1)} all-gather(bf16[8,256]{1,0:T(8,128)(2,1)} %param.9), channel_id=1, replica_groups=mesh['dp'=16,'feat'=16] {'dp'}, dimensions={1}, use_global_device_ids=true | all-gather | bytes 69632 | tf_op jit(solution)/shard_map/all_gather | solution.py:42
  74.3 29.4 %multiply_convert_fusion.2 = bf16[4096,512]{1,0:T(8,128)(2,1)S(1)} fusion(bf16[4096,256]{1,0:T(8,128)(2,1)} %all-gather.5.cloned.1.call-done, bf16[256,512]{1,0:T(8,128)(2,1)} %param.6, f32[512]{0:T(512)} %param.7), kind=kOutput, calls=%fused_computation.2 | convolution fusion | flops 1080033280 | bytes 6555648 | tf_op jit(solution)/shard_map/dot_general | solution.py:11
  103.7 1.9 copy-done.3
  105.7 1.3 convolution_bitcast_fusion.13
  106.9 7.7 %all-gather.7.cloned.1.call-done = bf16[256,8192]{1,0:T(8,128)(2,1)} async-done(((bf16[256,512]{1,0:T(8,128)(2,1)}), bf16[256,8192]{1,0:T(8,128)(2,1)}) %all-gather.7.cloned.1.call-update) | async-done | bytes 4194320 | tf_op jit(solution)/shard_map/all_gather | solution.py:45
  114.6 59.9 %multiply_convert_fusion.clone.6 = bf16[1024,4096]{1,0:T(8,128)(2,1)} fusion(bf16[4096,256]{1,0:T(8,128)(2,1)S(1)} %copy-done.6, f32[1024]{0:T(1024)S(1)} %dynamic_slice.23, bf16[256,8192]{1,0:T(8,128)(2,1)} %all-gather.7.cloned.1.call-done, s32[]{:T(128)S(6)} %select_n.32), kind=kOutput, calls=%fused_computation.clone.clone.clone.2 | convolution fusion | flops 2160066560 | bytes 11014148 | tf_op jit(solution)/shard_map/dot_general | solution.py:11
  174.5 26.7 %fusion = f32[1024,1024]{0,1:T(8,128)S(1)} fusion(bf16[1024,4096]{1,0:T(8,128)(2,1)} %multiply_convert_fusion.clone.6), kind=kOutput, calls=%fused_computation.3 | convolution fusion | flops 8589934592 | bytes 12582912 | tf_op jit(solution)/shard_map/dot_general | solution.py:16
  201.2 1.9 copy-done.1
  203.1 2.4 fusion.2
  205.5 5.3 %copy.11 = f32[1,1024,1024]{2,1,0:T(8,128)} copy(f32[1,1024,1024]{1,2,0:T(8,128)} %fusion.2) | data formatting | bytes 8388608 | tf_op jit(solution)/shard_map/stack | solution.py:70
  210.9 4.2 fusion.1
  215.1 1.9 copy-done.2
  217.0 11.7 %custom-call.67 = f32[1,128,128]{2,1,0:T(8,128)S(1)} custom-call(f32[1,128,128]{2,1,0:T(8,128)S(1)} %cholesky.585), custom_call_target="Cholesky" | custom-call | tf_op jit(solution)/shard_map/jit(cholesky)/cholesky | solution.py:71
  228.8 2.5 cholesky.249
  231.3 9.8 %custom-call.68 = f32[1,1,128,128]{2,3,1,0:T(8,128)S(1)} custom-call(f32[1,1,128,128]{3,2,1,0:T(8,128)S(1)} %get-tuple-element.24), custom_call_target="InvertDiagBlocksLowerTriangular" | custom-call | tf_op jit(solution)/shard_map/jit(cholesky)/cholesky | solution.py:71
  241.1 2.4 constant_dynamic-update-slice_fusion.7
  243.5 1.5 fusion.5
  245.0 11.7 %custom-call.69 = f32[1,128,128]{2,1,0:T(8,128)S(1)} custom-call(f32[1,128,128]{2,1,0:T(8,128)S(1)} %cholesky.589), custom_call_target="Cholesky" | custom-call | tf_op jit(solution)/shard_map/jit(cholesky)/cholesky | solution.py:71
  256.8 0.6 select_reduce_fusion.6
  257.4 10.2 %custom-call.70 = f32[1,1,128,128]{2,3,1,0:T(8,128)S(1)} custom-call(f32[1,1,128,128]{3,2,1,0:T(8,128)S(1)} %get-tuple-element.21), custom_call_target="InvertDiagBlocksLowerTriangular" | custom-call | tf_op jit(solution)/shard_map/jit(cholesky)/cholesky | solution.py:71
  267.6 1.2 fusion.6
  268.8 2.1 fusion.8
  271.0 11.7 %custom-call.71 = f32[1,128,128]{2,1,0:T(8,128)S(1)} custom-call(f32[1,128,128]{2,1,0:T(8,128)S(1)} %cholesky.594), custom_call_target="Cholesky" | custom-call | tf_op jit(solution)/shard_map/jit(cholesky)/cholesky | solution.py:71
  282.7 0.6 select_reduce_fusion.5
  283.3 9.8 %custom-call.72 = f32[1,1,128,128]{2,3,1,0:T(8,128)S(1)} custom-call(f32[1,1,128,128]{3,2,1,0:T(8,128)S(1)} %get-tuple-element.18), custom_call_target="InvertDiagBlocksLowerTriangular" | custom-call | tf_op jit(solution)/shard_map/jit(cholesky)/cholesky | solution.py:71
  293.1 1.2 fusion.7
  294.3 2.3 fusion.10
  296.6 11.9 %custom-call.73 = f32[1,128,128]{2,1,0:T(8,128)S(1)} custom-call(f32[1,128,128]{2,1,0:T(8,128)S(1)} %cholesky.599), custom_call_target="Cholesky" | custom-call | tf_op jit(solution)/shard_map/jit(cholesky)/cholesky | solution.py:71
  308.5 0.6 select_reduce_fusion.4
  309.2 9.8 %custom-call.74 = f32[1,1,128,128]{2,3,1,0:T(8,128)S(1)} custom-call(f32[1,1,128,128]{3,2,1,0:T(8,128)S(1)} %get-tuple-element.15), custom_call_target="InvertDiagBlocksLowerTriangular" | custom-call | tf_op jit(solution)/shard_map/jit(cholesky)/cholesky | solution.py:71
  319.0 1.1 fusion.9
  320.1 2.3 fusion.11
  322.4 11.7 %custom-call.75 = f32[1,128,128]{2,1,0:T(8,128)S(1)} custom-call(f32[1,128,128]{2,1,0:T(8,128)S(1)} %cholesky.604), custom_call_target="Cholesky" | custom-call | tf_op jit(solution)/shard_map/jit(cholesky)/cholesky | solution.py:71
  334.1 0.6 select_reduce_fusion.3
  334.8 9.8 %custom-call.76 = f32[1,1,128,128]{2,3,1,0:T(8,128)S(1)} custom-call(f32[1,1,128,128]{3,2,1,0:T(8,128)S(1)} %get-tuple-element.12), custom_call_target="InvertDiagBlocksLowerTriangular" | custom-call | tf_op jit(solution)/shard_map/jit(cholesky)/cholesky | solution.py:71
  344.6 1.3 fusion.12
  345.9 2.3 fusion.13
  348.1 11.7 %custom-call.77 = f32[1,128,128]{2,1,0:T(8,128)S(1)} custom-call(f32[1,128,128]{2,1,0:T(8,128)S(1)} %cholesky.609), custom_call_target="Cholesky" | custom-call | tf_op jit(solution)/shard_map/jit(cholesky)/cholesky | solution.py:71
  359.9 0.6 select_reduce_fusion.2
  360.5 9.8 %custom-call.78 = f32[1,1,128,128]{2,3,1,0:T(8,128)S(1)} custom-call(f32[1,1,128,128]{3,2,1,0:T(8,128)S(1)} %get-tuple-element.9), custom_call_target="InvertDiagBlocksLowerTriangular" | custom-call | tf_op jit(solution)/shard_map/jit(cholesky)/cholesky | solution.py:71
  370.3 0.9 fusion.14
  371.2 2.0 fusion.15
  373.3 11.7 %custom-call.79 = f32[1,128,128]{2,1,0:T(8,128)S(1)} custom-call(f32[1,128,128]{2,1,0:T(8,128)S(1)} %cholesky.614), custom_call_target="Cholesky" | custom-call | tf_op jit(solution)/shard_map/jit(cholesky)/cholesky | solution.py:71
  385.0 0.6 select_reduce_fusion.1
  385.6 10.2 %custom-call.80 = f32[1,1,128,128]{2,3,1,0:T(8,128)S(1)} custom-call(f32[1,1,128,128]{3,2,1,0:T(8,128)S(1)} %get-tuple-element.6), custom_call_target="InvertDiagBlocksLowerTriangular" | custom-call | tf_op jit(solution)/shard_map/jit(cholesky)/cholesky | solution.py:71
  395.8 0.8 fusion.16
  396.7 1.8 fusion.17
  398.4 11.7 %custom-call.81 = f32[1,128,128]{2,1,0:T(8,128)S(1)} custom-call(f32[1,128,128]{2,1,0:T(8,128)S(1)} %fusion.17), custom_call_target="Cholesky" | custom-call | tf_op jit(solution)/shard_map/jit(cholesky)/cholesky | solution.py:71
  410.1 0.6 select_reduce_fusion
  410.8 0.7 compare_reduce_fusion.5
  411.5 0.6 compare_reduce_fusion.4
  412.1 0.7 compare_reduce_fusion.3
  412.8 0.7 compare_reduce_fusion.2
  413.5 0.7 compare_reduce_fusion.1
  414.2 0.6 compare_reduce_fusion
  414.8 0.6 compare_reduce_fusion.6
  420.5 30.2 %multiply_convert_fusion.1.clone.4 = bf16[512,4096]{1,0:T(8,128)(2,1)S(1)} fusion(bf16[4096,256]{1,0:T(8,128)(2,1)S(1)} %copy-done.6, f32[512]{0:T(512)S(1)} %dynamic_slice.21, bf16[256,8192]{1,0:T(8,128)(2,1)} %all-gather.7.cloned.1.call-done, s32[]{:T(128)S(6)} %select_n.29), kind=kOutput, calls=%fused_computation.1.clone.clone.clone.1 | convolution fusion | flops 1080033280 | bytes 6555652 | tf_op jit(solution)/shard_map/dot_general | solution.py:11
  450.7 3.4 convolution_add_fusion
  454.1 1.6 fusion.4
  (26 shorter events, 0.2 us)
Async XLA Ops:
  7.2 67.1 %all-gather.5.cloned.1.call-start = ((), (), s32[]{:S(2)}) async-start(), calls=%async_computation | async-start | bytes 2228224 | tf_op jit(solution)/shard_map/all_gather | solution.py:41
  7.9 106.7 %all-gather.7.cloned.1.call-start = ((), (), s32[]{:S(2)}) async-start(), calls=%async_computation.1 | async-start | bytes 4456448 | tf_op jit(solution)/shard_map/all_gather | solution.py:45
  103.7 2.0 copy-start.3
  105.7 9.0 %copy-start.6 = (bf16[4096,256]{1,0:T(8,128)(2,1)S(1)}, bf16[4096,256]{1,0:T(8,128)(2,1)}, u32[]{:S(2)}) copy-start(bf16[4096,256]{1,0:T(8,128)(2,1)} %all-gather.5.cloned.1.call-done) | copy-start | bytes 6291460
  201.2 1.9 copy-start.1
  215.1 1.9 copy-start.2
  420.5 30.2 %copy-start.4 = (bf16[4096,512]{1,0:T(8,128)(2,1)S(1)}, bf16[4096,512]{1,0:T(8,128)(2,1)}, u32[]{:S(2)}) copy-start(bf16[4096,512]{1,0:T(8,128)(2,1)} %copy-done.3) | copy-start | bytes 12582916
  420.5 30.2 %copy-start.5 = (f32[512]{0:T(512)S(1)}, f32[512]{0:T(512)}, u32[]{:S(2)}) copy-start(f32[512]{0:T(512)} %param.8) | copy-start | bytes 6148
  450.7 3.4 copy-start
Sparse Core Ops, SparseCore 0:
  9.8 42.3 all-gather.4
  54.6 59.9 all-gather.6
where the time goes:
time: 472 us; the launch traced here: 463 us
  other arithmetic  181 us (38%)
  matrix products  174 us (37%)
  blocking collectives  65.5 us (14%)
  between operations  19.6 us (4%)
  local copies, waits for them, and re-layouts  13.8 us (3%)
  waiting for transfers between devices  9.11 us (2%)
    another operation x30, other arithmetic, shards(): factors_all = jnp.linalg.cholesky(stacked).reshape(window, FB)  172 us
    dot_general x3, matrix products, features(): jnp.dot(rows, freq_cols, preferred_element_type=jnp.float32) + phase_cols  119 us
    dot_general x2, matrix products, cross(): lax.dot_general(left, right, (((0,), (0,)), ((), ())), preferred_element_...  30.1 us
    all_gather x1, blocking collectives, shards(): lax.all_gather(phase, 'feat', axis=0, tiled=True)  23.4 us
    another operation x14, matrix products, shards(): factors_all = jnp.linalg.cholesky(stacked).reshape(window, FB)  23.3 us
    all_gather x1, blocking collectives, shards(): lax.all_gather(ridge, 'feat', axis=0, tiled=True)  21.7 us
    all_gather x1, blocking collectives, shards(): lax.all_gather(targets, 'dp', axis=1, tiled=True)  20.4 us
  transfers between devices with their start and end apart: 2, of which 1 were waited for; matrix products, arithmetic and copies ran while one was open for 7% of the time, Pallas kernels for 0%

commit v1 on v0

--- a/solution.py
+++ b/solution.py
@@ -39,7 +39,9 @@
     scale = math.sqrt(2.0 / (points.shape[0] * data_count))
     points_all, targets_all = (
         lax.all_gather(points, "dp", axis=0, tiled=True),
-        lax.all_gather(targets, "dp", axis=1, tiled=True),
+        jnp.concatenate(
+            lax.all_to_all(jnp.stack([targets] * lax.axis_size("dp")), "dp", 0, 0), axis=1
+        ),
     )
     freqs_wide, phase_all, ridge_all = (
         lax.all_gather(freqs.astype(jnp.float32), "feat", axis=1, tiled=True),

time: 472 us -> 472 us (level)
  blocking collectives: 65.5 us -> 45.1 us
  waiting for transfers between devices: 9.11 us -> 18.3 us
  starting transfers between devices: 0.08 us -> 8.64 us
    all_gather x1 -> x0, blocking collectives: 20.4 us -> none  [shards(): lax.all_gather(targets, 'dp', axis=1, tiled=True)]
    all_gather x1, waiting for transfers between devices: 7.72 us -> 16.9 us  [shards(): lax.all_gather(freqs.astype(jnp.float32), 'feat', axis=1, tiled=True)]
    all_to_all x0 -> x1, starting transfers between devices: none -> 8.57 us  [shards(): lax.all_to_all(jnp.stack([targets] * lax.axis_size('dp')), 'dp', 0, 0)]
  transfers between devices with their start and end apart: 2 -> 3, of which waited for: 1 -> 1; matrix products, arithmetic and copies ran while one was open for 7% -> 8% of each run, Pallas kernels for 0% -> 0%
where the time goes in v1:
time: 472 us; the launch traced here: 463 us
  other arithmetic  181 us (38%)
  matrix products  177 us (38%)
  blocking collectives  45.1 us (10%)
  between operations  19.6 us (4%)
  waiting for transfers between devices  18.3 us (4%)
  local copies, waits for them, and re-layouts  13.1 us (3%)
  starting transfers between devices  8.64 us (2%)
    another operation x30, other arithmetic, shards(): factors_all = jnp.linalg.cholesky(stacked).reshape(window, FB)  172 us
    dot_general x3, matrix products, features(): jnp.dot(rows, freq_cols, preferred_element_type=jnp.float32) + phase_cols  120 us
    dot_general x2, matrix products, cross(): lax.dot_general(left, right, (((0,), (0,)), ((), ())), preferred_element_...  30.1 us
    all_gather x1, blocking collectives, shards(): lax.all_gather(phase, 'feat', axis=0, tiled=True)  23.4 us
    another operation x14, matrix products, shards(): factors_all = jnp.linalg.cholesky(stacked).reshape(window, FB)  23.3 us
    all_gather x1, blocking collectives, shards(): lax.all_gather(ridge, 'feat', axis=0, tiled=True)  21.7 us
    all_gather x1, waiting for transfers between devices, shards(): lax.all_gather(freqs.astype(jnp.float32), 'feat', axis=1, tiled=True)  16.9 us
  transfers between devices with their start and end apart: 3, of which 1 were waited for; matrix products, arithmetic and copies ran while one was open for 8% of the time, Pallas kernels for 0%

profile of v1, /device:TPU:2, one launch (start us, length us, event | category | flops | bytes accessed | tf_op | source)
XLA Modules:
  0.0 462.7 jit_solution(10866653751592048242)
XLA Ops:
  7.2 0.7 all-gather.5.cloned.1.call-update
  7.9 0.7 all-gather.7.cloned.1.call-update
  8.6 1.3 stack.4
  10.0 8.6 %all-to-all-start = ((bf16[16,8,256]{2,1,0:T(8,128)(2,1)}), bf16[16,8,256]{2,1,0:T(8,128)(2,1)S(1)}, u32[]{:S(2)}, u32[]{:S(2)}) async-start(bf16[16,8,256]{2,1,0:T(8,128)(2,1)} %stack.4), calls=%async_computation | async-start | bytes 131072 | tf_op jit(solution)/shard_map/all_to_all | solution.py:43
  18.6 23.4 %all-gather = f32[16,1,512]{2,1,0:T(1,128)S(1)} all-gather(f32[1,1,512]{2,1,0:T(1,128)} %bitcast.192), channel_id=1, replica_groups=mesh['dp'=16,'feat'=16] {'feat'}, dimensions={0}, use_global_device_ids=true | all-gather | bytes 34816 | tf_op jit(solution)/shard_map/all_gather | solution.py:48
  42.0 0.1 dynamic_slice.21
  42.1 21.7 %all-gather.1 = f32[16,1,512]{2,1,0:T(1,128)S(1)} all-gather(f32[1,1,512]{2,1,0:T(1,128)} %bitcast.193), channel_id=1, replica_groups=mesh['dp'=16,'feat'=16] {'feat'}, dimensions={0}, use_global_device_ids=true | all-gather | bytes 34816 | tf_op jit(solution)/shard_map/all_gather | solution.py:49
  63.9 30.1 %multiply_convert_fusion.2 = bf16[4096,512]{1,0:T(8,128)(2,1)} fusion(bf16[4096,256]{1,0:T(8,128)(2,1)} %all-gather.5.cloned.1.call-done, bf16[256,512]{1,0:T(8,128)(2,1)} %param.6, f32[512]{0:T(512)} %param.7), kind=kOutput, calls=%fused_computation.2 | convolution fusion | flops 1080033280 | bytes 6555648 | tf_op jit(solution)/shard_map/dot_general | solution.py:11
  94.0 3.6 convolution_bitcast_fusion.13
  97.6 16.9 %all-gather.7.cloned.1.call-done = bf16[256,8192]{1,0:T(8,128)(2,1)} async-done(((bf16[256,512]{1,0:T(8,128)(2,1)}), bf16[256,8192]{1,0:T(8,128)(2,1)}) %all-gather.7.cloned.1.call-update) | async-done | bytes 4194320 | tf_op jit(solution)/shard_map/all_gather | solution.py:47
  114.5 59.9 %multiply_convert_fusion.clone.6 = bf16[1024,4096]{1,0:T(8,128)(2,1)} fusion(bf16[4096,256]{1,0:T(8,128)(2,1)S(1)} %copy-done.5, f32[1024]{0:T(1024)S(1)} %dynamic_slice.23, bf16[256,8192]{1,0:T(8,128)(2,1)} %all-gather.7.cloned.1.call-done, s32[]{:T(128)S(6)} %select_n.32), kind=kOutput, calls=%fused_computation.clone.clone.clone.2 | convolution fusion | flops 2160066560 | bytes 11014148 | tf_op jit(solution)/shard_map/dot_general | solution.py:11
  174.4 26.7 %fusion = f32[1024,1024]{0,1:T(8,128)S(1)} fusion(bf16[1024,4096]{1,0:T(8,128)(2,1)} %multiply_convert_fusion.clone.6), kind=kOutput, calls=%fused_computation.3 | convolution fusion | flops 8589934592 | bytes 12582912 | tf_op jit(solution)/shard_map/dot_general | solution.py:16
  201.1 1.9 copy-done.1
  203.0 2.4 fusion.2
  205.4 5.3 %copy.11 = f32[1,1024,1024]{2,1,0:T(8,128)} copy(f32[1,1024,1024]{1,2,0:T(8,128)} %fusion.2) | data formatting | bytes 8388608 | tf_op jit(solution)/shard_map/stack | solution.py:72
  210.8 4.2 fusion.1
  215.0 1.9 copy-done.2
  216.9 11.7 %custom-call.67 = f32[1,128,128]{2,1,0:T(8,128)S(1)} custom-call(f32[1,128,128]{2,1,0:T(8,128)S(1)} %cholesky.585), custom_call_target="Cholesky" | custom-call | tf_op jit(solution)/shard_map/jit(cholesky)/cholesky | solution.py:73
  228.7 2.5 cholesky.249
  231.2 9.8 %custom-call.68 = f32[1,1,128,128]{2,3,1,0:T(8,128)S(1)} custom-call(f32[1,1,128,128]{3,2,1,0:T(8,128)S(1)} %get-tuple-element.24), custom_call_target="InvertDiagBlocksLowerTriangular" | custom-call | tf_op jit(solution)/shard_map/jit(cholesky)/cholesky | solution.py:73
  241.0 2.4 constant_dynamic-update-slice_fusion.7
  243.4 1.5 fusion.5
  244.9 11.7 %custom-call.69 = f32[1,128,128]{2,1,0:T(8,128)S(1)} custom-call(f32[1,128,128]{2,1,0:T(8,128)S(1)} %cholesky.589), custom_call_target="Cholesky" | custom-call | tf_op jit(solution)/shard_map/jit(cholesky)/cholesky | solution.py:73
  256.6 0.6 select_reduce_fusion.6
  257.3 10.2 %custom-call.70 = f32[1,1,128,128]{2,3,1,0:T(8,128)S(1)} custom-call(f32[1,1,128,128]{3,2,1,0:T(8,128)S(1)} %get-tuple-element.21), custom_call_target="InvertDiagBlocksLowerTriangular" | custom-call | tf_op jit(solution)/shard_map/jit(cholesky)/cholesky | solution.py:73
  267.5 1.2 fusion.6
  268.7 2.1 fusion.8
  270.8 11.7 %custom-call.71 = f32[1,128,128]{2,1,0:T(8,128)S(1)} custom-call(f32[1,128,128]{2,1,0:T(8,128)S(1)} %cholesky.594), custom_call_target="Cholesky" | custom-call | tf_op jit(solution)/shard_map/jit(cholesky)/cholesky | solution.py:73
  282.5 0.6 select_reduce_fusion.5
  283.2 9.8 %custom-call.72 = f32[1,1,128,128]{2,3,1,0:T(8,128)S(1)} custom-call(f32[1,1,128,128]{3,2,1,0:T(8,128)S(1)} %get-tuple-element.18), custom_call_target="InvertDiagBlocksLowerTriangular" | custom-call | tf_op jit(solution)/shard_map/jit(cholesky)/cholesky | solution.py:73
  293.0 1.2 fusion.7
  294.2 2.3 fusion.10
  296.5 11.9 %custom-call.73 = f32[1,128,128]{2,1,0:T(8,128)S(1)} custom-call(f32[1,128,128]{2,1,0:T(8,128)S(1)} %cholesky.599), custom_call_target="Cholesky" | custom-call | tf_op jit(solution)/shard_map/jit(cholesky)/cholesky | solution.py:73
  308.4 0.6 select_reduce_fusion.4
  309.0 9.8 %custom-call.74 = f32[1,1,128,128]{2,3,1,0:T(8,128)S(1)} custom-call(f32[1,1,128,128]{3,2,1,0:T(8,128)S(1)} %get-tuple-element.15), custom_call_target="InvertDiagBlocksLowerTriangular" | custom-call | tf_op jit(solution)/shard_map/jit(cholesky)/cholesky | solution.py:73
  318.9 1.1 fusion.9
  320.0 2.3 fusion.11
  322.3 11.7 %custom-call.75 = f32[1,128,128]{2,1,0:T(8,128)S(1)} custom-call(f32[1,128,128]{2,1,0:T(8,128)S(1)} %cholesky.604), custom_call_target="Cholesky" | custom-call | tf_op jit(solution)/shard_map/jit(cholesky)/cholesky | solution.py:73
  334.0 0.6 select_reduce_fusion.3
  334.7 9.8 %custom-call.76 = f32[1,1,128,128]{2,3,1,0:T(8,128)S(1)} custom-call(f32[1,1,128,128]{3,2,1,0:T(8,128)S(1)} %get-tuple-element.12), custom_call_target="InvertDiagBlocksLowerTriangular" | custom-call | tf_op jit(solution)/shard_map/jit(cholesky)/cholesky | solution.py:73
  344.5 1.3 fusion.12
  345.7 2.3 fusion.13
  348.0 11.7 %custom-call.77 = f32[1,128,128]{2,1,0:T(8,128)S(1)} custom-call(f32[1,128,128]{2,1,0:T(8,128)S(1)} %cholesky.609), custom_call_target="Cholesky" | custom-call | tf_op jit(solution)/shard_map/jit(cholesky)/cholesky | solution.py:73
  359.7 0.6 select_reduce_fusion.2
  360.4 9.8 %custom-call.78 = f32[1,1,128,128]{2,3,1,0:T(8,128)S(1)} custom-call(f32[1,1,128,128]{3,2,1,0:T(8,128)S(1)} %get-tuple-element.9), custom_call_target="InvertDiagBlocksLowerTriangular" | custom-call | tf_op jit(solution)/shard_map/jit(cholesky)/cholesky | solution.py:73
  370.2 0.9 fusion.14
  371.1 2.0 fusion.15
  373.2 11.7 %custom-call.79 = f32[1,128,128]{2,1,0:T(8,128)S(1)} custom-call(f32[1,128,128]{2,1,0:T(8,128)S(1)} %cholesky.614), custom_call_target="Cholesky" | custom-call | tf_op jit(solution)/shard_map/jit(cholesky)/cholesky | solution.py:73
  384.9 0.6 select_reduce_fusion.1
  385.5 10.2 %custom-call.80 = f32[1,1,128,128]{2,3,1,0:T(8,128)S(1)} custom-call(f32[1,1,128,128]{3,2,1,0:T(8,128)S(1)} %get-tuple-element.6), custom_call_target="InvertDiagBlocksLowerTriangular" | custom-call | tf_op jit(solution)/shard_map/jit(cholesky)/cholesky | solution.py:73
  395.7 0.8 fusion.16
  396.5 1.8 fusion.17
  398.3 11.7 %custom-call.81 = f32[1,128,128]{2,1,0:T(8,128)S(1)} custom-call(f32[1,128,128]{2,1,0:T(8,128)S(1)} %fusion.17), custom_call_target="Cholesky" | custom-call | tf_op jit(solution)/shard_map/jit(cholesky)/cholesky | solution.py:73
  410.0 0.6 select_reduce_fusion
  410.7 0.7 compare_reduce_fusion.5
  411.4 0.6 compare_reduce_fusion.4
  412.0 0.7 compare_reduce_fusion.3
  412.7 0.7 compare_reduce_fusion.2
  413.4 0.7 compare_reduce_fusion.1
  414.0 0.6 compare_reduce_fusion
  414.7 0.6 compare_reduce_fusion.6
  420.4 30.2 %multiply_convert_fusion.1.clone.4 = bf16[512,4096]{1,0:T(8,128)(2,1)S(1)} fusion(bf16[4096,256]{1,0:T(8,128)(2,1)S(1)} %copy-done.5, f32[512]{0:T(512)S(1)} %dynamic_slice.21, bf16[256,8192]{1,0:T(8,128)(2,1)} %all-gather.7.cloned.1.call-done, s32[]{:T(128)S(6)} %select_n.29), kind=kOutput, calls=%fused_computation.1.clone.clone.clone.1 | convolution fusion | flops 1080033280 | bytes 6555652 | tf_op jit(solution)/shard_map/dot_general | solution.py:11
  450.6 3.4 convolution_add_fusion
  454.0 1.6 fusion.4
  (26 shorter events, 0.2 us)
Async XLA Ops:
  7.2 56.7 %all-gather.5.cloned.1.call-start = ((), (), s32[]{:S(2)}) async-start(), calls=%async_computation.1 | async-start | bytes 2228224 | tf_op jit(solution)/shard_map/all_gather | solution.py:41
  7.9 106.6 %all-gather.7.cloned.1.call-start = ((), (), s32[]{:S(2)}) async-start(), calls=%async_computation.2 | async-start | bytes 4456448 | tf_op jit(solution)/shard_map/all_gather | solution.py:47
  10.0 84.0 %all-to-all-start = ((bf16[16,8,256]{2,1,0:T(8,128)(2,1)}), bf16[16,8,256]{2,1,0:T(8,128)(2,1)S(1)}, u32[]{:S(2)}, u32[]{:S(2)}) async-start(bf16[16,8,256]{2,1,0:T(8,128)(2,1)} %stack.4), calls=%async_computation | async-start | bytes 131072 | tf_op jit(solution)/shard_map/all_to_all | solution.py:43
  94.0 20.5 %copy-start.5 = (bf16[4096,256]{1,0:T(8,128)(2,1)S(1)}, bf16[4096,256]{1,0:T(8,128)(2,1)}, u32[]{:S(2)}) copy-start(bf16[4096,256]{1,0:T(8,128)(2,1)} %all-gather.5.cloned.1.call-done) | copy-start | bytes 6291460
  201.1 1.9 copy-start.1
  215.0 1.9 copy-start.2
  420.4 30.2 %copy-start.3 = (bf16[4096,512]{1,0:T(8,128)(2,1)S(1)}, bf16[4096,512]{1,0:T(8,128)(2,1)}, u32[]{:S(2)}) copy-start(bf16[4096,512]{1,0:T(8,128)(2,1)} %multiply_convert_fusion.2) | copy-start | bytes 12582916
  420.4 30.2 %copy-start.4 = (f32[512]{0:T(512)S(1)}, f32[512]{0:T(512)}, u32[]{:S(2)}) copy-start(f32[512]{0:T(512)} %param.8) | copy-start | bytes 6148
  450.6 3.4 copy-start
Sparse Core Ops, SparseCore 0:
  9.8 42.3 all-gather.4
  54.6 59.8 all-gather.6
